TPU v7x, 128 devices: a whole 4x4x4 slice. The times are simulated.
128 devices in a mesh: tm: 8 (over y, core), ep: 16 (over x, z).
Axes of the slice: x: 4, y: 4, z: 4, core: 2. Of those that a mesh axis runs over, the one named last changes fastest.
Arguments:
- observations: bfloat16 [1024, 128, 1024], P('ep', 'tm'), may hold values from -6 to 6
- input_weight: bfloat16 [1024, 2048], replicated, may hold values from -0.1875 to 0.1875
- hidden_weight: bfloat16 [512, 2048], replicated, may hold values from -0.25 to 0.25
- gate_bias: float32 [2048], replicated, may hold values from -3 to 3
- forget_bias: float32 [512], replicated, may hold values from 0 to 5
- episode_ids: int32 [2048], P('ep'), may hold values from 0 to 63
- start_steps: int32 [2048], P('ep'), may hold values from 0 to 127
- priorities: int32 [2048], P('ep'), may hold values from 20 to 999
Outputs:
- train_rows: bfloat16 [2048, 128, 1024], P('ep', 'tm')
- start_state: bfloat16 [2048, 2, 512], P('ep')
- sample_weights: bfloat16 [2048], P('ep')
Inputs may be any that keep to these rules, and one draw needn't show every extreme that they name: `episode_ids`: slot index inside the storage shard that sampled the sequence.
All inputs are finite; a program needn't handle non-finite values.
Results may differ from a plain program's by a relative error of at most 0.009.
Values may be sent and summed in bfloat16 or wider, within the bound.
No kernel may reach another device: no remote copies, remote signals or barrier semaphores. Data moves between devices by JAX's collectives and lax.ppermute only.
A program may use at most 64 MiB of HBM per device.

v0:
```python
import jax
import jax.numpy as jnp
from jax import lax
from jax.sharding import Mesh
from jax.sharding import PartitionSpec as P

STEPS = 128
BURN = 40
UNROLL = 80
EP = ("ep_0", "ep_1")
IMPORTANCE = 0.6


def split_up(x, dim, devices):
    before, after = (x.shape[:dim], x.shape[dim + 1 :])
    return jnp.moveaxis(x.reshape(*before, devices, -1, *after), dim, 0)


def sum_at_owner(x, axis, dim):
    devices = lax.axis_size(axis)
    tiles = lax.all_to_all(split_up(x, dim, devices), axis, 0, 0, tiled=True)
    return jnp.sum(tiles.astype(jnp.float32), axis=0)


def one_axis_at_a_time(x, axes):
    for axis in axes:
        x = lax.pmax(x, axis)
    return x


def sent_together(arrays, axis, split_dim, concat_dim, along):
    columns = [a.reshape(*a.shape[:along], -1) for a in arrays]
    both = jnp.concatenate(columns, axis=along)
    whole, at, gathered = (
        lax.all_to_all(both, axis, split_axis=split_dim, concat_axis=concat_dim, tiled=True),
        0,
        [],
    )
    for a, column in zip(arrays, columns):
        piece = whole[..., at : at + column.shape[along]]
        gathered.append(piece.reshape(*piece.shape[:along], *a.shape[along:]))
        at += column.shape[along]
    return tuple(gathered)


def joined_along(tiles, dim):
    tiles = jnp.moveaxis(tiles, 0, dim)
    lengths = tiles.shape
    return tiles.reshape(*lengths[:dim], lengths[dim] * lengths[dim + 1], *lengths[dim + 2 :])


def sent_to_all(x, axis):
    copies = jnp.broadcast_to(x, (lax.axis_size(axis), *x.shape))
    return lax.all_to_all(copies, axis, split_axis=0, concat_axis=0, tiled=True)


def collect(x, axis, dim):
    return joined_along(sent_to_all(x, axis), dim)


def lstm_step(state_pair, projected, hidden_weight, gate_bias, forget_bias):
    hidden, cell_state = state_pair
    hidden_width = hidden.shape[-1]
    gate_sum = (
        projected
        + jnp.dot(hidden.astype(jnp.bfloat16), hidden_weight, preferred_element_type=jnp.float32)
        + gate_bias
    )
    ingate = gate_sum[:, :hidden_width]
    forget = gate_sum[:, hidden_width : 2 * hidden_width]
    candidate = gate_sum[:, 2 * hidden_width : 3 * hidden_width]
    outgate = gate_sum[:, 3 * hidden_width :]
    cell_state = jax.nn.sigmoid(forget + forget_bias) * cell_state + jax.nn.sigmoid(
        ingate
    ) * jnp.tanh(candidate)
    hidden = jax.nn.sigmoid(outgate) * jnp.tanh(cell_state)
    return (hidden, cell_state)


def body(
    observations,
    input_weight,
    hidden_weight,
    gate_bias,
    forget_bias,
    episode_ids,
    start_steps,
    priorities,
):
    shard_steps = observations.shape[1]
    seq_count = episode_ids.shape[0]
    hidden_width = hidden_weight.shape[0]
    time_shards = lax.axis_size("tm")
    position = lax.axis_index("tm")
    stored_rows = observations[episode_ids]
    local_steps = position * shard_steps + jnp.arange(shard_steps, dtype=jnp.int32)
    offsets = (local_steps[None, :] - start_steps[:, None]) % STEPS
    own_count = seq_count // time_shards
    whole_slots = lax.all_to_all(stored_rows, "tm", split_axis=0, concat_axis=1, tiled=True)
    own_starts = lax.dynamic_slice_in_dim(start_steps, position * own_count, own_count)
    burn_steps = (own_starts[None, :] + jnp.arange(BURN, dtype=jnp.int32)[:, None]) % STEPS
    own_index = jnp.broadcast_to(jnp.arange(own_count, dtype=jnp.int32)[None, :], burn_steps.shape)
    burn_inputs = whole_slots[own_index, burn_steps]
    burn_projected = jnp.dot(
        burn_inputs.reshape(BURN * own_count, burn_inputs.shape[2]),
        input_weight,
        preferred_element_type=jnp.float32,
    ).reshape(BURN, own_count, -1)

    def warm(state_pair, projected_now):
        return (lstm_step(state_pair, projected_now, hidden_weight, gate_bias, forget_bias), None)

    blank_own = jnp.zeros((own_count, hidden_width), jnp.float32)
    (own_hidden, own_cell), _ = lax.scan(warm, (blank_own, blank_own), burn_projected, unroll=4)
    own_pair = jnp.stack([own_hidden, own_cell], axis=1)
    final_pair = lax.dynamic_update_slice_in_dim(
        jnp.zeros((seq_count, 2, hidden_width), jnp.float32), own_pair, position * own_count, 0
    )
    start_state = sum_at_owner(final_pair.astype(jnp.bfloat16), "tm", 2).astype(jnp.bfloat16)
    train_mask = (offsets - BURN) % STEPS < UNROLL
    sent_rows = jnp.where(train_mask[:, :, None], stored_rows, jnp.zeros((), jnp.bfloat16))
    raw_weight = jnp.exp(-IMPORTANCE * jnp.log(priorities.astype(jnp.float32))).astype(jnp.bfloat16)
    peak_weight = one_axis_at_a_time(jnp.max(raw_weight.astype(jnp.float32)), EP)
    outgoing = (raw_weight.astype(jnp.float32) / peak_weight).astype(jnp.bfloat16)
    moved_rows, moved_state, moved_weights = sent_together(
        (sent_rows, start_state, outgoing), EP, 0, 0, 1
    )
    moved_state = collect(moved_state, "tm", 2)
    return (moved_rows, moved_state, moved_weights)


def solution(mesh):
    torus = Mesh(mesh.devices.reshape(mesh.shape["tm"], 4, 4), ("tm", "ep_0", "ep_1"))
    return jax.shard_map(
        body,
        mesh=torus,
        in_specs=(P(EP, "tm", None), P(), P(), P(), P(), P(EP), P(EP), P(EP)),
        out_specs=(P(EP, "tm", None), P(EP, None, None), P(EP)),
        check_vma=False,
    )
```

profile of v0, /device:TPU:1, one launch (start us, length us, event | category | flops | bytes accessed | tf_op | source)
XLA Modules:
  0.0 274.5 jit_solution(11965095968492109559)
XLA Ops:
  2.2 2.8 %gather_fusion = bf16[128,16,1024]{2,1,0:T(8,128)(2,1)} fusion(bf16[64,16,1024]{2,1,0:T(8,128)(2,1)S(1)} %copy-done, s32[1024]{0:T(1024)S(1)} %pad_clamp_fusion), kind=kCustom, calls=%fused_computation | custom fusion | bytes 8389120 | tf_op jit(solution)/shard_map/gather | solution.py:95
  5.1 6.1 %all-to-all-start = ((bf16[128,16,1024]{2,1,0:T(8,128)(2,1)}), bf16[128,16,1024]{2,1,0:T(8,128)(2,1)}, u32[]{:S(2)}, u32[]{:S(2)}) async-start(bf16[128,16,1024]{2,1,0:T(8,128)(2,1)} %gather_fusion), calls=%async_computation | async-start | bytes 8388608 | tf_op jit(solution)/shard_map/all_to_all | solution.py:99
  11.8 10.0 %pmax.14 = f32[]{:T(128)} all-reduce(bf16[]{:T(256)} %convert_reduce_fusion), channel_id=1, replica_groups=mesh['tm'=8,'ep_0'=4,'ep_1'=4] {'ep_0'}, use_global_device_ids=true, to_apply=%region_4.5 | all-reduce | flops 1 | bytes 6 | tf_op jit(solution)/shard_map/pmax | solution.py:27
  22.1 37.9 %all-to-all-done = bf16[128,16,1024]{2,1,0:T(8,128)(2,1)} async-done(((bf16[128,16,1024]{2,1,0:T(8,128)(2,1)}), bf16[128,16,1024]{2,1,0:T(8,128)(2,1)}, u32[]{:S(2)}, u32[]{:S(2)}) %all-to-all-start) | async-done | bytes 4194336 | tf_op jit(solution)/shard_map/all_to_all | solution.py:99
  59.9 5.0 %copy.28 = bf16[8,16,16,1024]{3,2,0,1:T(8,128)(2,1)} copy(bf16[8,16,16,1024]{3,2,1,0:T(8,128)(2,1)} %bitcast) | data formatting | bytes 8388608 | tf_op jit(solution)/shard_map/all_to_all | solution.py:99
  64.9 15.3 %gather_fusion.1 = bf16[640,1024]{1,0:T(8,128)(2,1)} fusion(bf16[16,128,1024]{2,1,0:T(8,128)(2,1)} %bitcast.61, s32[640]{0:T(1024)S(1)} %reshape.199), kind=kCustom, calls=%fused_computation.1 | custom fusion | bytes 2626560 | tf_op jit(solution)/shard_map/gather | solution.py:103
  80.3 7.8 %fusion.75 = f32[10,4,16,2048]{3,2,1,0:T(8,128)} fusion(bf16[10,4,16,1024]{3,2,1,0:T(8,128)(2,1)} %bitcast.67, bf16[1024,2048]{1,0:T(8,128)(2,1)} %param.11), kind=kOutput, calls=%fused_computation.100 | convolution fusion | flops 2684354560 | bytes 10747904 | tf_op jit(solution)/shard_map/dot_general | solution.py:104
  88.1 81.5 %while.13 = (s32[]{:T(128)}, bf16[16,512]{1,0:T(8,128)(2,1)S(1)}, f32[16,512]{1,0:T(8,128)S(1)}, f32[10,4,16,2048]{3,2,1,0:T(8,128)}, bf16[512,2048]{1,0:T(8,128...) while((s32[]{:T(128)}, bf16[16,512]{1,0:T(8,128)(2,1)S(1)}, ...), condition=%wide.region_1.2_spmd.clone, body=%wide.region_0.1_spmd.clone.sunk | while | flops 134987776 | bytes 10395840 | solution.py:114
  90.2 2.0 fusion.118
  92.2 2.0 fusion.120
  94.2 2.0 fusion.122
  96.3 2.0 fusion.116
  98.3 2.0 fusion.118
  100.3 2.0 fusion.120
  102.4 2.0 fusion.122
  104.4 2.0 fusion.116
  112.6 2.0 fusion.116
  120.7 2.0 fusion.116
  128.9 2.0 fusion.116
  137.1 2.0 fusion.116
  145.2 2.0 fusion.116
  153.4 2.0 fusion.116
  161.5 2.0 fusion.116
  172.3 3.4 %all-to-all-start.1 = ((bf16[8,128,2,64]{1,3,2,0:T(8,128)(2,1)}), bf16[8,128,2,64]{1,3,2,0:T(8,128)(2,1)S(1)}, u32[]{:S(2)}, u32[]{:S(2)}) async-start(bf16[8,128,2,64]{1,3,2,0:T(8,128)(2,1)} %copy.30), calls=%async_computation.1 | async-start | bytes 524288 | tf_op jit(solution)/shard_map/all_to_all | solution.py:21
  175.8 3.8 %broadcast_select_fusion = bf16[128,16,1024]{2,1,0:T(8,128)(2,1)} fusion(bf16[128,16,1024]{2,1,0:T(8,128)(2,1)} %gather_fusion, pred[128,16]{1,0:T(8,128)(4,1)S(1)} %fusion.79), kind=kLoop, calls=%fused_computation.102 | loop fusion | flops 2097152 | bytes 8390656 | tf_op jit(solution)/shard_map/jit(_where)/select_n | solution.py:121
  179.6 10.4 %pmax.15 = f32[]{:T(128)} all-reduce(f32[]{:T(128)} %pmax.14), channel_id=1, replica_groups=mesh['tm'=8,'ep_0'=4,'ep_1'=4] {'ep_1'}, use_global_device_ids=true, to_apply=%region_5.6 | all-reduce | flops 1 | bytes 8 | tf_op jit(solution)/shard_map/pmax | solution.py:27
  190.0 7.4 %select_n.64 = bf16[16,8,16384]{2,1,0:T(8,128)(2,1)} reshape(bf16[128,16,1024]{2,1,0:T(8,128)(2,1)} %broadcast_select_fusion) | data formatting | bytes 8388608 | tf_op jit(solution)/shard_map/jit(_where)/select_n | solution.py:121
  198.6 2.4 pad_maximum_fusion
  201.0 53.7 %all_to_all.37 = bf16[16,8,16513]{2,1,0:T(8,128)(2,1)S(1)} all-to-all(bf16[16,8,16513]{2,1,0:T(8,128)(2,1)S(1)} %pad_maximum_fusion), channel_id=1, replica_groups=mesh['tm'=8,'ep_0'=4,'ep_1'=4] {'ep_0','ep_1'}, dimensions={0} | all-to-all | bytes 8454656 | tf_op jit(solution)/shard_map/all_to_all | solution.py:35
  257.5 7.5 %all-to-all-start.3 = ((bf16[8,128,2,64]{1,3,2,0:T(8,128)(2,1)}), bf16[8,128,2,64]{1,3,2,0:T(8,128)(2,1)S(1)}, u32[]{:S(2)}, u32[]{:S(2)}) async-start(bf16[8,128,2,64]{1,3,2,0:T(8,128)(2,1)} %broadcast_in_dim.32), calls=%async_computation.3 | async-start | bytes 524288 | tf_op jit(solution)/shard_map/all_to_all | solution.py:54
  265.0 2.5 slice.116
  267.5 4.8 %copy.39 = bf16[16,8,16,1024]{3,2,1,0:T(8,128)(2,1)} copy(bf16[16,8,16,1024]{3,1,2,0:T(8,128)(2,1)S(1)} %bitcast.65) | data formatting | bytes 8388608
  (105 shorter events, 62.8 us)
Async XLA Ops:
  0.6 1.6 copy-start
  5.1 6.1 %copy-start.5 = (s32[128]{0:T(128)S(1)}, s32[128]{0:T(128)}, u32[]{:S(2)}) copy-start(s32[128]{0:T(128)} %param.17) | copy-start | bytes 1540
  5.1 16.7 %copy-start.4 = (s32[128]{0:T(128)S(1)}, s32[128]{0:T(128)}, u32[]{:S(2)}) copy-start(s32[128]{0:T(128)} %param.16) | copy-start | bytes 1540
  5.1 54.9 %all-to-all-start = ((bf16[128,16,1024]{2,1,0:T(8,128)(2,1)}), bf16[128,16,1024]{2,1,0:T(8,128)(2,1)}, u32[]{:S(2)}, u32[]{:S(2)}) async-start(bf16[128,16,1024]{2,1,0:T(8,128)(2,1)} %gather_fusion), calls=%async_computation | async-start | bytes 8388608 | tf_op jit(solution)/shard_map/all_to_all | solution.py:99
  80.3 7.8 %copy-start.2 = (f32[2048]{0:T(1024)S(1)}, f32[2048]{0:T(1024)}, u32[]{:S(2)}) copy-start(f32[2048]{0:T(1024)} %param.13) | copy-start | bytes 24580
  80.3 7.8 %copy-start.3 = (f32[512]{0:T(512)S(1)}, f32[512]{0:T(512)}, u32[]{:S(2)}) copy-start(f32[512]{0:T(512)} %param.14) | copy-start | bytes 6148
  172.3 26.0 %all-to-all-start.1 = ((bf16[8,128,2,64]{1,3,2,0:T(8,128)(2,1)}), bf16[8,128,2,64]{1,3,2,0:T(8,128)(2,1)S(1)}, u32[]{:S(2)}, u32[]{:S(2)}) async-start(bf16[8,128,2,64]{1,3,2,0:T(8,128)(2,1)} %copy.30), calls=%async_computation.1 | async-start | bytes 524288 | tf_op jit(solution)/shard_map/all_to_all | solution.py:21
  254.6 2.0 copy-start.1
  257.5 16.1 %all-to-all-start.3 = ((bf16[8,128,2,64]{1,3,2,0:T(8,128)(2,1)}), bf16[8,128,2,64]{1,3,2,0:T(8,128)(2,1)S(1)}, u32[]{:S(2)}, u32[]{:S(2)}) async-start(bf16[8,128,2,64]{1,3,2,0:T(8,128)(2,1)} %broadcast_in_dim.32), calls=%async_computation.3 | async-start | bytes 524288 | tf_op jit(solution)/shard_map/all_to_all | solution.py:54
where the time goes:
time: 277 us; the launch traced here: 275 us
  matrix products  87.2 us (31%)
  blocking collectives  74 us (27%)
  local copies, waits for them, and re-layouts  46.9 us (17%)
  waiting for transfers between devices  37.9 us (14%)
  starting transfers between devices  17.1 us (6%)
  other arithmetic  10.3 us (4%)
    dot_general x40, matrix products, lstm_step(): jnp.dot(hidden.astype(jnp.bfloat16), hidden_weight, preferred_element_typ...  79.3 us
    all_to_all x1, blocking collectives, sent_together(): lax.all_to_all(both, axis, split_axis=split_dim, concat_axis=concat_dim,...  53.7 us
    all_to_all x1, waiting for transfers between devices, body(): lax.all_to_all(stored_rows, 'tm', split_axis=0, concat_axis=1, tiled=True)  37.9 us
    pmax x2, blocking collectives, one_axis_at_a_time(): x = lax.pmax(x, axis)  20.3 us
    gather x1, local copies, waits for them, and re-layouts, body(): burn_inputs = whole_slots[own_index, burn_steps]  15.3 us
    unnamed x14, local copies, waits for them, and re-layouts  8.41 us
    dot_general x1, matrix products, body(): jnp.dot(burn_inputs.reshape(BURN * own_count, burn_inputs.shape[2]), inpu...  7.84 us
    all_to_all x1, starting transfers between devices, sent_to_all(): return lax.all_to_all(copies, axis, split_axis=0, concat_axis=0, tiled=True)  7.54 us
  transfers between devices with their start and end apart: 3, of which 1 were waited for; matrix products, arithmetic and copies ran while one was open for 8% of the time, Pallas kernels for 0%

commit v1 on v0

--- a/solution.py
+++ b/solution.py
@@ -9,6 +9,34 @@
 UNROLL = 80
 EP = ("ep_0", "ep_1")
 IMPORTANCE = 0.6
+
+
+def unite_teams(own_rows, d0, message):
+    o_now = own_rows.shape
+    fresh = own_rows.reshape(*o_now[:d0], message, o_now[d0] // message, *o_now[d0 + 1 :])
+    answer = jnp.moveaxis(fresh, d0, 0)
+    return answer
+
+
+def series_launch(incoming_x, join_dim):
+    passed = list(incoming_x.shape[1:])
+    passed[join_dim] *= incoming_x.shape[0]
+    current_arr = jnp.moveaxis(incoming_x, 0, join_dim).reshape(passed)
+    return current_arr
+
+
+def arrange_steps_all(inp, row_axis, vals, q_in):
+    now = lax.axis_size(row_axis)
+    piece_now, y = (now, lax.axis_index(row_axis))
+    shaped = unite_teams(inp, vals, piece_now)
+    pile = [shaped[y]]
+    for pp in [*range(1, piece_now)]:
+        f_now = shaped[y ^ pp]
+        work_now = lax.ppermute(f_now, row_axis, [(i0, i0 ^ pp) for i0 in range(piece_now)])
+        pile.append(work_now)
+    shaped = jnp.stack(pile)[y ^ jnp.arange(piece_now)]
+    e_next = series_launch(shaped, q_in)
+    return e_next
 
 
 def split_up(x, dim, devices):
@@ -96,7 +124,7 @@
     local_steps = position * shard_steps + jnp.arange(shard_steps, dtype=jnp.int32)
     offsets = (local_steps[None, :] - start_steps[:, None]) % STEPS
     own_count = seq_count // time_shards
-    whole_slots = lax.all_to_all(stored_rows, "tm", split_axis=0, concat_axis=1, tiled=True)
+    whole_slots = arrange_steps_all(stored_rows, "tm", 0, 1)
     own_starts = lax.dynamic_slice_in_dim(start_steps, position * own_count, own_count)
     burn_steps = (own_starts[None, :] + jnp.arange(BURN, dtype=jnp.int32)[:, None]) % STEPS
     own_index = jnp.broadcast_to(jnp.arange(own_count, dtype=jnp.int32)[None, :], burn_steps.shape)

time: 277 us -> 265 us (0.957)
  matrix products: 87.2 us -> 59.7 us
  local copies, waits for them, and re-layouts: 46.9 us -> 58.1 us
  starting transfers between devices: 17.1 us -> 23.3 us
    ppermute x0 -> x7, waiting for transfers between devices: none -> 38.8 us  [arrange_steps_all(): lax.ppermute(f_now, row_axis, [(i0, i0 ^ pp) for i0 in range(piece_now)])]
    all_to_all x1 -> x0, waiting for transfers between devices: 37.9 us -> none  [body(): lax.all_to_all(stored_rows, 'tm', split_axis=0, concat_axis=1, tiled=True)]
    dot_general x40, matrix products: 79.3 us -> 51.8 us  [lstm_step(): jnp.dot(hidden.astype(jnp.bfloat16), hidden_weight, preferred_element_typ...]
    ppermute x0 -> x7, starting transfers between devices: none -> 11.4 us  [arrange_steps_all(): lax.ppermute(f_now, row_axis, [(i0, i0 ^ pp) for i0 in range(piece_now)])]
    all_to_all x1 -> x0, starting transfers between devices: 6.09 us -> none  [body(): lax.all_to_all(stored_rows, 'tm', split_axis=0, concat_axis=1, tiled=True)]
    unnamed x14 -> x24, local copies, waits for them, and re-layouts: 8.41 us -> 13.5 us
    all_to_all x1 -> x0, local copies, waits for them, and re-layouts: 4.99 us -> none  [body(): lax.all_to_all(stored_rows, 'tm', split_axis=0, concat_axis=1, tiled=True)]
    gather x0 -> x1, local copies, waits for them, and re-layouts: none -> 4.99 us  [arrange_steps_all(): shaped = jnp.stack(pile)[y ^ jnp.arange(piece_now)]]
  transfers between devices with their start and end apart: 3 -> 9, of which waited for: 1 -> 4; matrix products, arithmetic and copies ran while one was open for 8% -> 10% of each run, Pallas kernels for 0% -> 0%
where the time goes in v1:
time: 265 us; the launch traced here: 263 us
  blocking collectives  71.7 us (27%)
  matrix products  59.7 us (23%)
  local copies, waits for them, and re-layouts  58.1 us (22%)
  waiting for transfers between devices  38.8 us (15%)
  starting transfers between devices  23.3 us (9%)
  other arithmetic  10.3 us (4%)
    all_to_all x1, blocking collectives, sent_together(): lax.all_to_all(both, axis, split_axis=split_dim, concat_axis=concat_dim,...  51.9 us
    dot_general x40, matrix products, lstm_step(): jnp.dot(hidden.astype(jnp.bfloat16), hidden_weight, preferred_element_typ...  51.8 us
    ppermute x7, waiting for transfers between devices, arrange_steps_all(): lax.ppermute(f_now, row_axis, [(i0, i0 ^ pp) for i0 in range(piece_now)])  38.8 us
    pmax x2, blocking collectives, one_axis_at_a_time(): x = lax.pmax(x, axis)  19.8 us
    unnamed x24, local copies, waits for them, and re-layouts  13.5 us
    ppermute x7, starting transfers between devices, arrange_steps_all(): lax.ppermute(f_now, row_axis, [(i0, i0 ^ pp) for i0 in range(piece_now)])  11.4 us
    gather x1, local copies, waits for them, and re-layouts, body(): burn_inputs = whole_slots[own_index, burn_steps]  11.4 us
    dot_general x1, matrix products, body(): jnp.dot(burn_inputs.reshape(BURN * own_count, burn_inputs.shape[2]), inpu...  7.91 us
  transfers between devices with their start and end apart: 9, of which 4 were waited for; matrix products, arithmetic and copies ran while one was open for 10% of the time, Pallas kernels for 0%

profile of v1, /device:TPU:1, one launch (start us, length us, event | category | flops | bytes accessed | tf_op | source)
XLA Modules:
  0.0 263.3 jit_solution(10469053987465969795)
XLA Ops:
  2.2 2.8 %gather_fusion = bf16[128,16,1024]{2,1,0:T(8,128)(2,1)} fusion(bf16[64,16,1024]{2,1,0:T(8,128)(2,1)S(1)} %copy-done, s32[1024]{0:T(1024)S(1)} %pad_clamp_fusion.1), kind=kCustom, calls=%fused_computation | custom fusion | bytes 8389120 | tf_op jit(solution)/shard_map/gather | solution.py:123
  5.1 4.3 %dynamic-slice_bitcast_fusion.4 = (bf16[16,16,1024]{2,1,0:T(8,128)(2,1)}, bf16[16,16,1024]{2,1,0:T(8,128)(2,1)}, bf16[16,16,1024]{2,1,0:T(8,128)(2,1)}, bf16[16,...) fusion(bf16[8,16,16,1024]{3,2,1,0:T(8,128)(2,1)} %bitcast.91, ...), kind=kLoop, calls=%fused_computation.111 | loop fusion | bytes 8388640 | tf_op jit(solution)/shard_map/squeeze | solution.py:34
  9.3 1.4 collective-permute-start
  10.7 1.4 collective-permute-start.1
  12.4 3.0 %collective-permute-start.3 = (bf16[16,16,1024]{2,1,0:T(8,128)(2,1)}, bf16[16,16,1024]{2,1,0:T(8,128)(2,1)S(1)}, u32[]{:S(2)}, u32[]{:S(2)}) collective-permute-start(bf16[16,16,1024]{2,1,0:T(8,128)(2,1)} %get-tuple-element.95), channel_id=1, source_target_pairs={{0,64},{16,80},{32,96},{48,112},{64,0},{80,16},{96,32},{112,48},{1... | collective-permute-start | bytes 1572872 | tf_op jit(solution)/shard_map/ppermute | solution.py:35
  16.6 9.3 %pmax.14 = f32[]{:T(128)} all-reduce(bf16[]{:T(256)} %convert_reduce_fusion), channel_id=1, replica_groups=mesh['tm'=8,'ep_0'=4,'ep_1'=4] {'ep_0'}, use_global_device_ids=true, to_apply=%region_4.5 | all-reduce | flops 1 | bytes 6 | tf_op jit(solution)/shard_map/pmax | solution.py:55
  26.0 2.8 %collective-permute-start.5 = (bf16[16,16,1024]{2,1,0:T(8,128)(2,1)}, bf16[16,16,1024]{2,1,0:T(8,128)(2,1)S(1)}, u32[]{:S(2)}, u32[]{:S(2)}) collective-permute-start(bf16[16,16,1024]{2,1,0:T(8,128)(2,1)} %get-tuple-element.93), channel_id=1, source_target_pairs={{0,96},{16,112},{32,64},{48,80},{64,32},{80,48},{96,0},{112,16},{1... | collective-permute-start | bytes 1572872 | tf_op jit(solution)/shard_map/ppermute | solution.py:35
  29.6 2.2 collective-permute-start.6
  32.7 4.0 %collective-permute-done.2 = bf16[16,16,1024]{2,1,0:T(8,128)(2,1)S(1)} collective-permute-done((bf16[16,16,1024]{2,1,0:T(8,128)(2,1)}, bf16[16,16,1024]{2,1,0:T(8,128)(2,1)S(1)}, u32[]{:S(2)}, u32[]{:S(2)}) %collective-permute-start.2) | collective-permute-done | bytes 524320 | tf_op jit(solution)/shard_map/ppermute | solution.py:35
  37.5 11.9 %collective-permute-done.3 = bf16[16,16,1024]{2,1,0:T(8,128)(2,1)S(1)} collective-permute-done((bf16[16,16,1024]{2,1,0:T(8,128)(2,1)}, bf16[16,16,1024]{2,1,0:T(8,128)(2,1)S(1)}, u32[]{:S(2)}, u32[]{:S(2)}) %collective-permute-start.3) | collective-permute-done | bytes 524320 | tf_op jit(solution)/shard_map/ppermute | solution.py:35
  50.3 10.7 %collective-permute-done.4 = bf16[16,16,1024]{2,1,0:T(8,128)(2,1)S(1)} collective-permute-done((bf16[16,16,1024]{2,1,0:T(8,128)(2,1)}, bf16[16,16,1024]{2,1,0:T(8,128)(2,1)S(1)}, u32[]{:S(2)}, u32[]{:S(2)}) %collective-permute-start.4) | collective-permute-done | bytes 524320 | tf_op jit(solution)/shard_map/ppermute | solution.py:35
  62.6 12.2 %collective-permute-done.6 = bf16[16,16,1024]{2,1,0:T(8,128)(2,1)S(1)} collective-permute-done((bf16[16,16,1024]{2,1,0:T(8,128)(2,1)}, bf16[16,16,1024]{2,1,0:T(8,128)(2,1)S(1)}, u32[]{:S(2)}, u32[]{:S(2)}) %collective-permute-start.6) | collective-permute-done | bytes 524320 | tf_op jit(solution)/shard_map/ppermute | solution.py:35
  75.7 5.0 %gather_fusion.1 = bf16[8,16,16,1024]{3,2,1,0:T(8,128)(2,1)} fusion(bf16[8,16,16,1024]{3,2,1,0:T(8,128)(2,1)} %bitcast_dynamic-update-slice_fusion, s32[1024]{0:T(1024)S(1)} %pad_clamp_fusion), kind=kCustom, calls=%fused_computation.1 | custom fusion | bytes 8388640 | tf_op jit(solution)/shard_map/gather | solution.py:37
  80.7 5.0 %copy.26 = bf16[16,8,16,1024]{3,2,1,0:T(8,128)(2,1)} copy(bf16[16,8,16,1024]{3,2,0,1:T(8,128)(2,1)} %bitcast.95) | data formatting | bytes 8388608 | tf_op jit(solution)/shard_map/transpose | solution.py:24
  85.7 11.4 %gather_fusion.2 = bf16[640,1024]{1,0:T(8,128)(2,1)} fusion(bf16[16,128,1024]{2,1,0:T(8,128)(2,1)} %bitcast.90, s32[640]{0:T(1024)S(1)} %reshape.231), kind=kCustom, calls=%fused_computation.2 | custom fusion | bytes 2626560 | tf_op jit(solution)/shard_map/gather | solution.py:131
  97.0 7.9 %fusion.75 = f32[10,4,16,2048]{3,2,1,0:T(8,128)} fusion(bf16[10,4,16,1024]{3,2,1,0:T(8,128)(2,1)} %bitcast.98, bf16[1024,2048]{1,0:T(8,128)(2,1)} %param.11), kind=kOutput, calls=%fused_computation.101 | convolution fusion | flops 2684354560 | bytes 10747904 | tf_op jit(solution)/shard_map/dot_general | solution.py:132
  105.0 54.0 %while.13 = (s32[]{:T(128)}, bf16[16,512]{1,0:T(8,128)(2,1)S(1)}, f32[16,512]{1,0:T(8,128)S(1)}, f32[10,4,16,2048]{3,2,1,0:T(8,128)}, bf16[512,2048]{1,0:T(8,128...) while((s32[]{:T(128)}, bf16[16,512]{1,0:T(8,128)(2,1)S(1)}, ...), condition=%wide.region_1.2_spmd.clone, body=%wide.region_0.1_spmd.clone.sunk | while | flops 134987776 | bytes 10395840 | solution.py:142
  110.4 1.3 fusion.117
  115.8 1.3 fusion.117
  121.2 1.3 fusion.117
  159.2 1.7 dynamic_update_slice.3
  161.6 4.3 %all-to-all-start = ((bf16[8,128,2,64]{1,3,2,0:T(8,128)(2,1)}), bf16[8,128,2,64]{1,3,2,0:T(8,128)(2,1)S(1)}, u32[]{:S(2)}, u32[]{:S(2)}) async-start(bf16[8,128,2,64]{1,3,2,0:T(8,128)(2,1)} %copy.28), calls=%async_computation | async-start | bytes 524288 | tf_op jit(solution)/shard_map/all_to_all | solution.py:49
  166.0 3.8 %broadcast_select_fusion = bf16[128,16,1024]{2,1,0:T(8,128)(2,1)} fusion(bf16[128,16,1024]{2,1,0:T(8,128)(2,1)} %gather_fusion, pred[128,16]{1,0:T(8,128)(4,1)S(1)} %fusion.79), kind=kLoop, calls=%fused_computation.103 | loop fusion | flops 2097152 | bytes 8390656 | tf_op jit(solution)/shard_map/jit(_where)/select_n | solution.py:149
  169.8 10.6 %pmax.15 = f32[]{:T(128)} all-reduce(f32[]{:T(128)} %pmax.14), channel_id=1, replica_groups=mesh['tm'=8,'ep_0'=4,'ep_1'=4] {'ep_1'}, use_global_device_ids=true, to_apply=%region_5.6 | all-reduce | flops 1 | bytes 8 | tf_op jit(solution)/shard_map/pmax | solution.py:55
  180.4 7.4 %select_n.98 = bf16[16,8,16384]{2,1,0:T(8,128)(2,1)} reshape(bf16[128,16,1024]{2,1,0:T(8,128)(2,1)} %broadcast_select_fusion) | data formatting | bytes 8388608 | tf_op jit(solution)/shard_map/jit(_where)/select_n | solution.py:149
  188.9 2.4 pad_maximum_fusion
  191.3 51.9 %all_to_all.19 = bf16[16,8,16513]{2,1,0:T(8,128)(2,1)S(1)} all-to-all(bf16[16,8,16513]{2,1,0:T(8,128)(2,1)S(1)} %pad_maximum_fusion), channel_id=1, replica_groups=mesh['tm'=8,'ep_0'=4,'ep_1'=4] {'ep_0','ep_1'}, dimensions={0} | all-to-all | bytes 8454656 | tf_op jit(solution)/shard_map/all_to_all | solution.py:63
  243.2 2.0 copy-done.3
  246.1 7.6 %all-to-all-start.2 = ((bf16[8,128,2,64]{1,3,2,0:T(8,128)(2,1)}), bf16[8,128,2,64]{1,3,2,0:T(8,128)(2,1)S(1)}, u32[]{:S(2)}, u32[]{:S(2)}) async-start(bf16[8,128,2,64]{1,3,2,0:T(8,128)(2,1)} %broadcast_in_dim.32), calls=%async_computation.2 | async-start | bytes 524288 | tf_op jit(solution)/shard_map/all_to_all | solution.py:82
  253.7 2.5 slice.118
  256.2 4.8 %copy.37 = bf16[16,8,16,1024]{3,2,1,0:T(8,128)(2,1)} copy(bf16[16,8,16,1024]{3,1,2,0:T(8,128)(2,1)S(1)} %bitcast.96) | data formatting | bytes 8388608
  261.0 1.4 slice_reduce_fusion
  (132 shorter events, 62.6 us)
Async XLA Ops:
  0.6 1.6 copy-start
  5.1 10.7 %copy-start.6 = (s32[128]{0:T(128)S(1)}, s32[128]{0:T(128)}, u32[]{:S(2)}) copy-start(s32[128]{0:T(128)} %param.16) | copy-start | bytes 1540
  5.1 10.9 %copy-start.7 = (s32[128]{0:T(128)S(1)}, s32[128]{0:T(128)}, u32[]{:S(2)}) copy-start(s32[128]{0:T(128)} %param.17) | copy-start | bytes 1540
  9.3 16.6 %collective-permute-start = (bf16[16,16,1024]{2,1,0:T(8,128)(2,1)}, bf16[16,16,1024]{2,1,0:T(8,128)(2,1)S(1)}, u32[]{:S(2)}, u32[]{:S(2)}) collective-permute-start(bf16[16,16,1024]{2,1,0:T(8,128)(2,1)} %get-tuple-element.98), channel_id=1, source_target_pairs={{0,16},{16,0},{32,48},{48,32},{64,80},{80,64},{96,112},{112,96},{1... | collective-permute-start | bytes 1572872 | tf_op jit(solution)/shard_map/ppermute | solution.py:35
  10.7 18.9 %collective-permute-start.1 = (bf16[16,16,1024]{2,1,0:T(8,128)(2,1)}, bf16[16,16,1024]{2,1,0:T(8,128)(2,1)S(1)}, u32[]{:S(2)}, u32[]{:S(2)}) collective-permute-start(bf16[16,16,1024]{2,1,0:T(8,128)(2,1)} %get-tuple-element.97), channel_id=1, source_target_pairs={{0,32},{16,48},{32,0},{48,16},{64,96},{80,112},{96,64},{112,80},{1... | collective-permute-start | bytes 1572872 | tf_op jit(solution)/shard_map/ppermute | solution.py:35
  12.1 24.5 %collective-permute-start.2 = (bf16[16,16,1024]{2,1,0:T(8,128)(2,1)}, bf16[16,16,1024]{2,1,0:T(8,128)(2,1)S(1)}, u32[]{:S(2)}, u32[]{:S(2)}) collective-permute-start(bf16[16,16,1024]{2,1,0:T(8,128)(2,1)} %get-tuple-element.96), channel_id=1, source_target_pairs={{0,48},{16,32},{32,16},{48,0},{64,112},{80,96},{96,80},{112,64},{1... | collective-permute-start | bytes 1572872 | tf_op jit(solution)/shard_map/ppermute | solution.py:35
  12.4 37.0 %collective-permute-start.3 = (bf16[16,16,1024]{2,1,0:T(8,128)(2,1)}, bf16[16,16,1024]{2,1,0:T(8,128)(2,1)S(1)}, u32[]{:S(2)}, u32[]{:S(2)}) collective-permute-start(bf16[16,16,1024]{2,1,0:T(8,128)(2,1)} %get-tuple-element.95), channel_id=1, source_target_pairs={{0,64},{16,80},{32,96},{48,112},{64,0},{80,16},{96,32},{112,48},{1... | collective-permute-start | bytes 1572872 | tf_op jit(solution)/shard_map/ppermute | solution.py:35
  15.5 45.5 %collective-permute-start.4 = (bf16[16,16,1024]{2,1,0:T(8,128)(2,1)}, bf16[16,16,1024]{2,1,0:T(8,128)(2,1)S(1)}, u32[]{:S(2)}, u32[]{:S(2)}) collective-permute-start(bf16[16,16,1024]{2,1,0:T(8,128)(2,1)} %get-tuple-element.94), channel_id=1, source_target_pairs={{0,80},{16,64},{32,112},{48,96},{64,16},{80,0},{96,48},{112,32},{1... | collective-permute-start | bytes 1572872 | tf_op jit(solution)/shard_map/ppermute | solution.py:35
  26.0 35.8 %collective-permute-start.5 = (bf16[16,16,1024]{2,1,0:T(8,128)(2,1)}, bf16[16,16,1024]{2,1,0:T(8,128)(2,1)S(1)}, u32[]{:S(2)}, u32[]{:S(2)}) collective-permute-start(bf16[16,16,1024]{2,1,0:T(8,128)(2,1)} %get-tuple-element.93), channel_id=1, source_target_pairs={{0,96},{16,112},{32,64},{48,80},{64,32},{80,48},{96,0},{112,16},{1... | collective-permute-start | bytes 1572872 | tf_op jit(solution)/shard_map/ppermute | solution.py:35
  29.6 45.3 %collective-permute-start.6 = (bf16[16,16,1024]{2,1,0:T(8,128)(2,1)}, bf16[16,16,1024]{2,1,0:T(8,128)(2,1)S(1)}, u32[]{:S(2)}, u32[]{:S(2)}) collective-permute-start(bf16[16,16,1024]{2,1,0:T(8,128)(2,1)} %get-tuple-element.92), channel_id=1, source_target_pairs={{0,112},{16,96},{32,80},{48,64},{64,48},{80,32},{96,16},{112,0},{1... | collective-permute-start | bytes 1572872 | tf_op jit(solution)/shard_map/ppermute | solution.py:35
  97.0 7.9 %copy-start.2 = (bf16[512,2048]{1,0:T(8,128)(2,1)S(1)}, bf16[512,2048]{1,0:T(8,128)(2,1)}, u32[]{:S(2)}) copy-start(bf16[512,2048]{1,0:T(8,128)(2,1)} %param.12) | copy-start | bytes 6291460
  97.0 7.9 %copy-start.4 = (f32[2048]{0:T(1024)S(1)}, f32[2048]{0:T(1024)}, u32[]{:S(2)}) copy-start(f32[2048]{0:T(1024)} %param.13) | copy-start | bytes 24580
  97.0 7.9 %copy-start.5 = (f32[512]{0:T(512)S(1)}, f32[512]{0:T(512)}, u32[]{:S(2)}) copy-start(f32[512]{0:T(512)} %param.14) | copy-start | bytes 6148
  161.6 27.0 %all-to-all-start = ((bf16[8,128,2,64]{1,3,2,0:T(8,128)(2,1)}), bf16[8,128,2,64]{1,3,2,0:T(8,128)(2,1)S(1)}, u32[]{:S(2)}, u32[]{:S(2)}) async-start(bf16[8,128,2,64]{1,3,2,0:T(8,128)(2,1)} %copy.28), calls=%async_computation | async-start | bytes 524288 | tf_op jit(solution)/shard_map/all_to_all | solution.py:49
  243.2 2.0 copy-start.3
  246.1 16.3 %all-to-all-start.2 = ((bf16[8,128,2,64]{1,3,2,0:T(8,128)(2,1)}), bf16[8,128,2,64]{1,3,2,0:T(8,128)(2,1)S(1)}, u32[]{:S(2)}, u32[]{:S(2)}) async-start(bf16[8,128,2,64]{1,3,2,0:T(8,128)(2,1)} %broadcast_in_dim.32), calls=%async_computation.2 | async-start | bytes 524288 | tf_op jit(solution)/shard_map/all_to_all | solution.py:82
  256.2 7.1 %copy-start.1 = (bf16[64,16,1024]{2,1,0:T(8,128)(2,1)S(1)}, bf16[64,16,1024]{2,1,0:T(8,128)(2,1)}, u32[]{:S(2)}) copy-start(bf16[64,16,1024]{2,1,0:T(8,128)(2,1)} %param.10) | copy-start | bytes 6291460
